TPU v7x, 256 devices: a whole 4x4x8 slice. The times are simulated.
256 devices in a mesh: variant: 4 (over y), sub: 64 (over x, z, core).
Axes of the slice: x: 4, y: 4, z: 8, core: 2. Of those that a mesh axis runs over, the one named last changes fastest.
Arguments:
- displacement: float32 [4, 6, 8192], P('variant', None, 'sub'), may hold values from -6 to 6
- neighbours: int32 [2, 8192], P(None, 'sub'), may hold values from 0 to 129, as said below
- micro_state: bfloat16 [4, 196608, 512], P('variant', 'sub'), may hold values from -6 to 6
- strain_loads: float32 [4, 6, 512], P('variant'), may hold values from -3 to 3
- stiffness: bfloat16 [4, 512, 512], P('variant'), may hold values from -0.25 to 0.25
- expand_weight: bfloat16 [4, 512, 2048], P('variant'), may hold values from -0.25 to 0.25
- contract_weight: bfloat16 [4, 2048, 512], P('variant'), may hold values from -0.125 to 0.125
- batch_route: int32 [4, 2, 1536], P('variant', None, 'sub'), may hold values from -1 to 63, as said below
- yield_flags: int32 [4, 196608], P('variant', 'sub'), may hold values 0 or 1
- readout: bfloat16 [4, 512], P('variant'), may hold values from -0.75 to 0.75
- external_force: float32 [4, 8192], P('variant', 'sub'), may hold values from -6 to 6
- coarse_inverse: bfloat16 [4, 8192, 8192], P('variant', 'sub'), may hold values from -0.0625 to 0.0625
Outputs:
- states_next: bfloat16 [4, 196608, 512], P('variant', 'sub')
- coarse_correction: float32 [4, 8192], P('variant', 'sub')
Inputs may be any that keep to these rules, and one draw needn't show every extreme that they name: `neighbours`: entry 0 is position i or i + 1 of macro point i within its device (i counted from 0 in the device), entry 1 is i + 1 or i + 2, and entry 1 exceeds entry 0; the first and last point of each device use i and i + 2. `batch_route`: entry 0 of a batch held by device s on sub is -1 or (s + d) % 64 for some d from 1 to 16, each d used by at most one batch of s; entry 1 is -1 where entry 0 is, else its slot there, 0 to 7. Batches sent to one device have different slots; every device receives at most 8 batches, and in every draw some device receives 8.
All inputs are finite; a program needn't handle non-finite values. No bound on the sum of `yield_flags` on one device may be relied on, other than what follows from the above.
Results may differ from a plain program's by a relative error of at most 0.0055.
Values may be sent and summed in bfloat16 or wider, within the bound.
A program may use at most 64 MiB of HBM per device.

v0:
```python
import jax
import jax.numpy as jnp
from jax import lax
from jax.sharding import PartitionSpec as P

BATCH = 128


def extended_2(x, sides, width):
    for axis, dim in sides:
        devices, length = (lax.axis_size(axis), x.shape[dim])
        up = [(i, (i + 1) % devices) for i in range(devices - 1)]
        down = [(j, i) for i, j in up]
        last = lax.slice_in_dim(x, length - width, length, axis=dim)
        first = lax.slice_in_dim(x, 0, width, axis=dim)
        before = lax.ppermute(last, axis, up)
        after = lax.ppermute(first, axis, down)
        x = jnp.concatenate([before, x, after], axis=dim)
    return x


def sent_to_all(x, axis):
    copies = jnp.broadcast_to(x, (lax.axis_size(axis), *x.shape))
    return lax.all_to_all(copies, axis, split_axis=0, concat_axis=0, tiled=True)


def laid_out(blocks, dim):
    blocks = jnp.moveaxis(blocks, 0, dim)
    dims = blocks.shape
    return blocks.reshape(*dims[:dim], dims[dim] * dims[dim + 1], *dims[dim + 2 :])


def gathered_copies(x, axis, dim):
    blocks = sent_to_all(x, axis)
    return laid_out(blocks, dim)


def plastic_update(row_block, expand_weight, contract_weight):
    hidden = jax.nn.silu(
        jnp.dot(row_block, expand_weight, preferred_element_type=jnp.float32)
    ).astype(jnp.bfloat16)
    return jnp.dot(hidden, contract_weight, preferred_element_type=jnp.float32).astype(jnp.bfloat16)


def on_device(
    displacement,
    neighbours,
    micro_state,
    strain_loads,
    stiffness,
    expand_weight,
    contract_weight,
    batch_route,
    yield_flags,
    readout,
    external_force,
    coarse_inverse,
):
    extended = extended_2(displacement, (("sub", 2),), 1)
    lower_value = jnp.take(extended[0], neighbours[0], axis=1)
    upper_value = jnp.take(extended[0], neighbours[1], axis=1)
    spacing = (neighbours[1] - neighbours[0]).astype(jnp.float32)
    strain = (upper_value - lower_value) / spacing
    state_rows = micro_state[0]
    row_count = state_rows.shape[0]
    per_point = row_count // strain.shape[1]
    per_row = jnp.repeat(strain, per_point, axis=1)
    trial_state = state_rows.astype(jnp.float32) + jnp.dot(
        per_row.T, strain_loads[0], precision=lax.Precision.HIGHEST
    )
    elastic = jnp.dot(
        trial_state.astype(jnp.bfloat16), stiffness[0], preferred_element_type=jnp.float32
    )
    elastic_half = elastic.astype(jnp.bfloat16)
    target = batch_route[0, 0]
    alive_batch = (target >= 0).astype(jnp.int32)
    correction = plastic_update(elastic_half, expand_weight[0], contract_weight[0]).astype(
        jnp.float32
    )
    weight_rows = (jnp.repeat(alive_batch, BATCH) * yield_flags[0]).astype(jnp.float32)
    next_state = (elastic + weight_rows[:, None] * correction).astype(jnp.bfloat16)
    projected = jnp.dot(next_state, readout[0], preferred_element_type=jnp.float32)
    averaged = jnp.mean(projected.reshape(-1, per_point), axis=1)
    residual = (external_force[0] - averaged).astype(jnp.bfloat16)[None, :]
    inverse_rows = coarse_inverse[0]
    coarse = jnp.dot(
        inverse_rows, gathered_copies(residual, "sub", 1)[0], preferred_element_type=jnp.float32
    )
    return (next_state[None], coarse[None])


def solution(mesh):
    return jax.shard_map(
        on_device,
        mesh=mesh,
        in_specs=(
            P("variant", None, "sub"),
            P(None, "sub"),
            P("variant", "sub", None),
            P("variant", None, None),
            P("variant", None, None),
            P("variant", None, None),
            P("variant", None, None),
            P("variant", None, "sub"),
            P("variant", "sub"),
            P("variant", None),
            P("variant", "sub"),
            P("variant", "sub", None),
        ),
        out_specs=(P("variant", "sub", None), P("variant", "sub")),
        check_vma=False,
    )
```

profile of v0, /device:TPU:1, one launch (start us, length us, event | category | flops | bytes accessed | tf_op | source)
XLA Modules:
  0.0 76.4 jit_solution(8920192543859124947)
XLA Ops:
  0.6 0.0 copy-start
  0.6 0.9 %fusion.24 = (f32[1,6,1]{2,0,1:T(1,128)S(1)}, f32[1,6,1]{2,0,1:T(1,128)S(1)}) fusion(f32[1,6,128]{2,0,1:T(1,128)} %param.14), kind=kLoop, calls=%fused_computation.39 | loop fusion | bytes 96 | tf_op jit(solution)/shard_map/slice | solution.py:14
  1.6 4.9 %collective-permute-start = (f32[1,6,1]{2,0,1:T(1,128)S(1)}, f32[1,6,1]{2,0,1:T(1,128)S(1)}, u32[]{:S(2)}, u32[]{:S(2)}) collective-permute-start(f32[1,6,1]{2,0,1:T(1,128)S(1)} %get-tuple-element.7), channel_id=1, source_target_pairs={{0,1},{1,2},{2,3},{3,4},{4,5},{5,6},{6,7},{7,8},{8,9},{9,10},{10,1... | collective-permute-start | bytes 80 | tf_op jit(solution)/shard_map/ppermute | solution.py:16
  6.5 1.9 %collective-permute-start.1 = (f32[1,6,1]{2,0,1:T(1,128)S(1)}, f32[1,6,1]{2,0,1:T(1,128)S(1)}, u32[]{:S(2)}, u32[]{:S(2)}) collective-permute-start(f32[1,6,1]{2,0,1:T(1,128)S(1)} %get-tuple-element.8), channel_id=1, source_target_pairs={{1,0},{2,1},{3,2},{4,3},{5,4},{6,5},{7,6},{8,7},{9,8},{10,9},{11,1... | collective-permute-start | bytes 80 | tf_op jit(solution)/shard_map/ppermute | solution.py:17
  8.4 0.8 convert_bitcast_fusion
  9.2 0.8 compare_and_fusion.1
  9.9 0.7 fusion.21
  10.6 0.8 %fusion.17 = f32[3072]{0:T(1024)S(1)} fusion(s32[3072]{0:T(1024)} %bitcast.63, s32[24]{0:T(128)S(1)} %fusion.21), kind=kLoop, calls=%fused_computation.21 | loop fusion | flops 6144 | bytes 24672 | tf_op jit(solution)/shard_map/convert_element_type | solution.py:80
  11.4 0.0 collective-permute-done
  11.4 0.0 collective-permute-done.1
  11.4 0.8 %pad_maximum_fusion = f32[1,6,130]{2,0,1:T(1,128)S(1)} fusion(f32[1,6,1]{2,0,1:T(1,128)S(1)} %collective-permute-done.1, f32[1,6,128]{2,0,1:T(1,128)} %param.14, f32[1,6,1]{2,0,1:T(1,128)S(1)} %collective-permute-done), kind=kLoop, calls=%fused_computation.22 | loop fusion | flops 1560 | bytes 6240 | tf_op jit(solution)/shard_map/concatenate | solution.py:18
  12.2 0.1 copy.26
  12.3 0.6 gather_fusion.1
  13.0 0.1 copy.28
  13.0 0.7 gather_fusion
  13.7 0.1 copy.27
  13.8 0.2 broadcast_in_dim.27
  13.9 0.2 reshape.33
  14.2 0.0 copy-start.1
  14.2 6.9 %fusion.3 = bf16[3072,512]{1,0:T(8,128)(2,1)S(1)} fusion(f32[6,3072]{1,0:T(8,128)S(1)} %reshape.33, bf16[1,3072,512]{2,1,0:T(8,128)(2,1)} %param.16, f32[1,6,512]{2,0,1:T(1,128)} %param.17), kind=kOutput, calls=%fused_computation.6 | convolution fusion | flops 117964800 | bytes 6377472 | tf_op jit(solution)/shard_map/dot_general | solution.py:68
  21.1 0.0 copy-done.1
  21.1 4.5 %fusion.12 = f32[3072,512]{1,0:T(8,128)} fusion(bf16[3072,512]{1,0:T(8,128)(2,1)S(1)} %fusion.3, bf16[1,512,512]{2,1,0:T(8,128)(2,1)S(1)} %copy-done.1), kind=kOutput, calls=%fused_computation.14 | convolution fusion | flops 1610612736 | bytes 9961472 | tf_op jit(solution)/shard_map/dot_general | solution.py:71
  25.6 0.0 copy-done
  25.6 0.0 copy-start.2
  25.6 21.2 %add_convert_fusion = bf16[3072,512]{1,0:T(8,128)(2,1)} fusion(f32[3072,512]{1,0:T(8,128)} %fusion.12, f32[3072]{0:T(1024)S(1)} %fusion.17, bf16[1,2048,512]{2,1,0:T(8,128)(2,1)S(1)} %copy-done, bf16[1,512,2048]{2,1,0:T(8,128)(2,1)} %param.19), kind=kOutput, calls=%fused_computation.7 | convolution fusion | flops 12925796352 | bytes 13643776 | tf_op jit(solution)/shard_map/dot_general | solution.py:42
  46.8 0.0 copy-start.3
  46.8 0.0 copy-done.2
  46.8 4.7 %fusion.19 = f32[1,128,24]{2,0,1:T(1,128)S(1)} fusion(bf16[128,24,512]{2,1,0:T(8,128)(2,1)} %bitcast.59, bf16[1,512]{1,0:T(2,128)(2,1)S(1)} %copy-done.2), kind=kOutput, calls=%fused_computation.29 | convolution fusion | flops 3145728 | bytes 3159040 | tf_op jit(solution)/shard_map/dot_general | solution.py:82
  51.5 0.1 copy.29
  51.6 0.0 copy-done.3
  51.7 22.0 %all_to_all.5 = bf16[64,1,128]{2,1,0:T(2,128)(2,1)S(1)} all-to-all(bf16[64,1,128]{2,1,0:T(2,128)(2,1)S(1)} %broadcast_in_dim.30), channel_id=1, replica_groups=mesh['variant'=4,'sub'=64] {'sub'}, dimensions={0} | all-to-all | bytes 32768 | tf_op jit(solution)/shard_map/all_to_all | solution.py:24
  73.7 2.8 %fusion.7 = f32[1,128]{1,0:T(1,128)} fusion(bf16[1,128,8192]{2,1,0:T(8,128)(2,1)} %param.25, bf16[64,1,128]{2,1,0:T(2,128)(2,1)S(1)} %all_to_all.5), kind=kOutput, calls=%fused_computation.10 | convolution fusion | flops 2097152 | bytes 2114048 | tf_op jit(solution)/shard_map/dot_general | solution.py:86
  (5 shorter events, 0.1 us)
Async XLA Ops:
  0.6 25.0 %copy-start = (bf16[1,2048,512]{2,1,0:T(8,128)(2,1)S(1)}, bf16[1,2048,512]{2,1,0:T(8,128)(2,1)}, u32[]{:S(2)}) copy-start(bf16[1,2048,512]{2,1,0:T(8,128)(2,1)} %param.20) | copy-start | bytes 6291460
  1.6 9.8 %collective-permute-start = (f32[1,6,1]{2,0,1:T(1,128)S(1)}, f32[1,6,1]{2,0,1:T(1,128)S(1)}, u32[]{:S(2)}, u32[]{:S(2)}) collective-permute-start(f32[1,6,1]{2,0,1:T(1,128)S(1)} %get-tuple-element.7), channel_id=1, source_target_pairs={{0,1},{1,2},{2,3},{3,4},{4,5},{5,6},{6,7},{7,8},{8,9},{9,10},{10,1... | collective-permute-start | bytes 80 | tf_op jit(solution)/shard_map/ppermute | solution.py:16
  6.5 4.9 %collective-permute-start.1 = (f32[1,6,1]{2,0,1:T(1,128)S(1)}, f32[1,6,1]{2,0,1:T(1,128)S(1)}, u32[]{:S(2)}, u32[]{:S(2)}) collective-permute-start(f32[1,6,1]{2,0,1:T(1,128)S(1)} %get-tuple-element.8), channel_id=1, source_target_pairs={{1,0},{2,1},{3,2},{4,3},{5,4},{6,5},{7,6},{8,7},{9,8},{10,9},{11,1... | collective-permute-start | bytes 80 | tf_op jit(solution)/shard_map/ppermute | solution.py:17
  14.2 6.9 %copy-start.1 = (bf16[1,512,512]{2,1,0:T(8,128)(2,1)S(1)}, bf16[1,512,512]{2,1,0:T(8,128)(2,1)}, u32[]{:S(2)}) copy-start(bf16[1,512,512]{2,1,0:T(8,128)(2,1)} %param.18) | copy-start | bytes 1572868
  25.6 21.2 %copy-start.2 = (bf16[1,512]{1,0:T(2,128)(2,1)S(1)}, bf16[1,512]{1,0:T(2,128)(2,1)}, u32[]{:S(2)}) copy-start(bf16[1,512]{1,0:T(2,128)(2,1)} %param.23) | copy-start | bytes 3076
  46.8 4.8 %copy-start.3 = (f32[1,128]{1,0:T(1,128)S(1)}, f32[1,128]{1,0:T(1,128)}, u32[]{:S(2)}) copy-start(f32[1,128]{1,0:T(1,128)} %param.24) | copy-start | bytes 1540
where the time goes:
time: 76.8 us; the launch traced here: 76.4 us
  matrix products  40.1 us (52%)
  blocking collectives  22 us (29%)
  starting transfers between devices  6.84 us (9%)
  other arithmetic  3.81 us (5%)
  local copies, waits for them, and re-layouts  2.98 us (4%)
    all_to_all x1, blocking collectives, sent_to_all(): return lax.all_to_all(copies, axis, split_axis=0, concat_axis=0, tiled=True)  22 us
    dot_general x1, matrix products, plastic_update(): jnp.dot(hidden, contract_weight, preferred_element_type=jnp.float32)  21.2 us
    dot_general x1, matrix products, on_device(): jnp.dot(per_row.T, strain_loads[0], precision=lax.Precision.HIGHEST)  6.93 us
    ppermute x1, starting transfers between devices, extended_2(): before = lax.ppermute(last, axis, up)  4.92 us
    dot_general x1, matrix products, on_device(): jnp.dot(next_state, readout[0], preferred_element_type=jnp.float32)  4.7 us
    dot_general x1, matrix products, on_device(): jnp.dot(trial_state.astype(jnp.bfloat16), stiffness[0], preferred_element...  4.45 us
    dot_general x1, matrix products, on_device(): jnp.dot(inverse_rows, gathered_copies(residual, 'sub', 1)[0], preferred_e...  2.76 us
    ppermute x1, starting transfers between devices, extended_2(): after = lax.ppermute(first, axis, down)  1.92 us
  transfers between devices with their start and end apart: 2, of which 0 were waited for; matrix products, arithmetic and copies ran while one was open for 4% of the time, Pallas kernels for 0%

commit v1 on v0

v1 whole, which is shorter than its diff:
```python
import functools

import jax
import jax.numpy as jnp
from jax import lax
from jax.experimental import pallas as pl
from jax.experimental.pallas import tpu as pltpu
from jax.sharding import PartitionSpec as P

BATCH = 128
RPP = 24
BATCHES = 24
POINTS = 128
ROWS = 3072
MODES = 512
HIDDEN = 2048
TILE = 384
TILES = ROWS // TILE
WINDOW = BATCH + 16
PACKED = 2048 + 256
F32, BF16, I32 = jnp.float32, jnp.bfloat16, jnp.int32
MESH = pl.DeviceIdType.MESH


def mm(a, b, dims=((1,), (0,)), precision=None):
    return lax.dot_general(a, b, (dims, ((), ())), precision=precision, preferred_element_type=F32)


def micro_kernel(
    route_ref, flags_ref, disp_ref, before_ref, after_ref, neigh_ref, loads_ref, readout_ref, force_ref,
    micro_hbm, stiff_hbm, expand_hbm, contract_hbm,
    next_hbm, resid_ref,
    states, stiff, expand, contract, elastic, packed, update, delta, slot_t, sums, offs_v, offs_s,
    in_sem, w_sem, out_sem, offs_sem,
):
    def tile_rows(t):
        return pl.ds(t * TILE, TILE)

    loads_in = [pltpu.make_async_copy(micro_hbm.at[tile_rows(t)], states.at[tile_rows(t)], in_sem.at[t]) for t in range(TILES)]
    stiff_in = pltpu.make_async_copy(stiff_hbm, stiff, w_sem.at[0])
    expand_in = pltpu.make_async_copy(expand_hbm, expand, w_sem.at[1])
    contract_in = pltpu.make_async_copy(contract_hbm, contract, w_sem.at[2])
    stiff_in.start()
    for copy in loads_in:
        copy.start()
    expand_in.start()
    contract_in.start()

    sub_i = lax.broadcasted_iota(I32, (128, 128), 0)
    lane_i = lax.broadcasted_iota(I32, (128, 128), 1)
    before_mask = (sub_i < lane_i).astype(BF16)
    flags = jnp.concatenate(
        [flags_ref[0:1, b * BATCH:(b + 1) * BATCH] for b in range(BATCHES)] + [jnp.zeros((128 - BATCHES, 128), I32)], axis=0
    ).astype(F32)
    flags_b = flags.astype(BF16)
    offs_v[...] = jnp.full((8, 128), -1, I32)
    offs_v[1:2, 0:BATCHES] = route_ref[0:1, :]
    alive = (offs_v[1:2, :] >= 0).astype(F32)
    totals = mm(jnp.ones((8, 128), BF16), flags_b, ((1,), (1,))) * alive
    offsets = mm(totals.astype(BF16), before_mask)
    offs_v[0:1, :] = offsets[0:1, :].astype(I32)
    offs_v[1:2, :] = alive.astype(I32)
    offs_copy = pltpu.make_async_copy(offs_v, offs_s, offs_sem)
    offs_copy.start()
    slot = jnp.where(flags > 0, mm(flags_b, before_mask), -1.0e6)
    slot_t[...] = slot.T
    slot_i = slot.astype(I32)

    disp = disp_ref[...]
    lane6 = lax.broadcasted_iota(I32, (6, 128), 1)
    prev = jnp.where(lane6 == 0, before_ref[...], pltpu.roll(disp, 1, 1))
    follow = jnp.where(lane6 == POINTS - 1, after_ref[...], pltpu.roll(disp, POINTS - 1, 1))
    low_i, high_i = neigh_ref[0:1, :], neigh_ref[1:2, :]
    here = lax.broadcasted_iota(I32, (1, 128), 1)
    lower = jnp.where(low_i == here, prev, disp)
    upper = jnp.where(high_i == here + 2, follow, disp)
    strain = (upper - lower) / (high_i - low_i).astype(F32)
    strain_t = jnp.concatenate([strain, jnp.zeros((122, 128), F32)], axis=0).T
    total = strain_t[:, 0:1] * loads_ref[0:1, :]
    for k in range(1, 6):
        total = total + strain_t[:, k:k + 1] * loads_ref[k:k + 1, :]
    delta[...] = total

    packed[0:16, :] = jnp.zeros((16, MODES), BF16)
    row_w = lax.broadcasted_iota(I32, (WINDOW, 128), 0)
    stiff_in.wait()
    offs_copy.wait()
    for t in range(TILES):
        loads_in[t].wait()
        shift = jnp.concatenate(
            [jnp.broadcast_to(delta[p:p + 1, :], (RPP, MODES)) for p in range(t * 16, t * 16 + 16)], axis=0
        )
        trial = (states[tile_rows(t), :].astype(F32) + shift).astype(BF16)
        rows = mm(trial, stiff[...])
        elastic[tile_rows(t), :] = rows
        half = rows.astype(BF16)
        for j in range(3):
            b = t * 3 + j
            off, live = offs_s[0, b], offs_s[1, b]
            base = pl.multiple_of((off // 16) * 16, 16)
            lead = jnp.where(live > 0, off - base, -1000000)
            pick = (row_w == slot_i[b:b + 1, :] + lead).astype(BF16)
            got = mm(pick, half[j * BATCH:(j + 1) * BATCH, :]).astype(BF16)
            packed[pl.ds(base, 16), :] = packed[pl.ds(base, 16), :] + got[0:16]
            packed[pl.ds(base + 16, BATCH), :] = got[16:]

    expand_in.wait()
    contract_in.wait()
    count = offs_s[0, BATCHES]
    packed[pl.ds(pl.multiple_of(((count + 15) // 16) * 16, 16), BATCH), :] = jnp.zeros((BATCH, MODES), BF16)

    def plastic(start, length):
        x = packed[pl.ds(start, length), :]
        acc = None
        for n in range(4):
            a = mm(x, expand[:, n * 512:(n + 1) * 512])
            h = (a * (0.5 + 0.5 * jnp.tanh(0.5 * a))).astype(BF16)
            part = mm(h, contract[n * 512:(n + 1) * 512, :])
            acc = part if acc is None else acc + part
        update[pl.ds(start, length), :] = acc.astype(BF16)

    whole = (count + 127) // 256

    @pl.loop(0, whole)
    def _(i):
        plastic(pl.multiple_of(i * 256, 256), 256)

    done = pl.multiple_of(whole * 256, 256)

    @pl.when(count > done)
    def _():
        plastic(done, 128)

    tail = pl.multiple_of(((count + 127) // 128) * 128, 128)
    update[pl.ds(tail, WINDOW), :] = jnp.zeros((WINDOW, MODES), BF16)

    lane_w = lax.broadcasted_iota(I32, (BATCH, WINDOW), 1).astype(F32)
    members = (
        lax.broadcasted_iota(I32, (16, TILE), 1) // RPP == lax.broadcasted_iota(I32, (16, TILE), 0)
    ).astype(BF16)
    copies_out = []
    for t in range(TILES):
        for j in range(3):
            b = t * 3 + j
            off, live = offs_s[0, b], offs_s[1, b]
            base = pl.multiple_of((off // 16) * 16, 16)
            lead = jnp.where(live > 0, off - base, -1000000).astype(F32)
            put = (slot_t[:, b:b + 1] + lead == lane_w).astype(BF16)
            back = mm(put, update[pl.ds(base, WINDOW), :])
            rows = pl.ds(b * BATCH, BATCH)
            states[rows, :] = (elastic[rows, :] + back).astype(BF16)
        copy = pltpu.make_async_copy(states.at[tile_rows(t)], next_hbm.at[tile_rows(t)], out_sem.at[t])
        copy.start()
        copies_out.append(copy)
        sums[t * 16:(t + 1) * 16, :] = mm(members, states[tile_rows(t), :])
    weighed = sums[...] * readout_ref[...].astype(F32)
    lanes = weighed[:, 0:128] + weighed[:, 128:256] + weighed[:, 256:384] + weighed[:, 384:512]
    mean = jnp.sum(lanes.T, axis=0, keepdims=True) / RPP
    resid_ref[...] = (force_ref[...] - mean).astype(BF16).astype(F32)
    for copy in copies_out:
        copy.wait()


def micro_step(route, flags, disp, before, after, neigh, loads, readout, force, micro, stiff, expand, contract):
    vmem = pl.BlockSpec(memory_space=pltpu.VMEM)
    hbm = pl.BlockSpec(memory_space=pl.ANY)
    return pl.pallas_call(
        micro_kernel,
        name="micro",
        out_shape=(jax.ShapeDtypeStruct((ROWS, MODES), BF16), jax.ShapeDtypeStruct((1, POINTS), F32)),
        in_specs=[vmem] * 9 + [hbm] * 4,
        out_specs=(hbm, vmem),
        scratch_shapes=[
            pltpu.VMEM((ROWS, MODES), BF16),
            pltpu.VMEM((MODES, MODES), BF16),
            pltpu.VMEM((MODES, HIDDEN), BF16),
            pltpu.VMEM((HIDDEN, MODES), BF16),
            pltpu.VMEM((ROWS, MODES), F32),
            pltpu.VMEM((PACKED, MODES), BF16),
            pltpu.VMEM((PACKED, MODES), BF16),
            pltpu.VMEM((POINTS, MODES), F32),
            pltpu.VMEM((128, 128), F32),
            pltpu.VMEM((POINTS, MODES), F32),
            pltpu.VMEM((8, 128), I32),
            pltpu.SMEM((8, 128), I32),
            pltpu.SemaphoreType.DMA((TILES,)),
            pltpu.SemaphoreType.DMA((3,)),
            pltpu.SemaphoreType.DMA((TILES,)),
            pltpu.SemaphoreType.DMA,
        ],
        cost_estimate=pl.CostEstimate(flops=10_000_000_000, bytes_accessed=11_000_000, transcendentals=2_000_000),
    )(route, flags, disp, before, after, neigh, loads, readout, force, micro, stiff, expand, contract)


def coarse_kernel(devices, resid_ref, inverse_hbm, out_ref, inverse, blocks, in_sem, send_sem, recv_sem):
    me = lax.axis_index("sub")
    load = pltpu.make_async_copy(inverse_hbm, inverse, in_sem)
    load.start()
    barrier = pltpu.get_barrier_semaphore()
    for d in range(1, devices):
        pl.semaphore_signal(barrier, inc=1, device_id={"sub": lax.rem(me + d, devices)}, device_id_type=MESH)
    pl.semaphore_wait(barrier, devices - 1)
    sends = []
    for d in range(1, devices):
        copy = pltpu.make_async_remote_copy(
            src_ref=resid_ref,
            dst_ref=blocks.at[me],
            send_sem=send_sem,
            recv_sem=recv_sem,
            device_id={"sub": lax.rem(me + d, devices)},
            device_id_type=MESH,
        )
        copy.start()
        sends.append(copy)
    blocks[me] = resid_ref[...]
    load.wait()
    everyone = blocks.at[pl.ds(0, devices - 1)]
    pltpu.make_async_copy(everyone, everyone, recv_sem).wait()
    acc = None
    for s in range(devices):
        part = inverse[:, s * POINTS:(s + 1) * POINTS].astype(F32) * blocks[s]
        acc = part if acc is None else acc + part
    out_ref[...] = jnp.sum(acc.T, axis=0, keepdims=True)
    pltpu.make_async_copy(everyone, everyone, send_sem).wait()


def coarse_step(resid, inverse, devices):
    return pl.pallas_call(
        functools.partial(coarse_kernel, devices),
        name="coarse",
        out_shape=jax.ShapeDtypeStruct((1, POINTS), F32),
        in_specs=[pl.BlockSpec(memory_space=pltpu.VMEM), pl.BlockSpec(memory_space=pl.ANY)],
        out_specs=pl.BlockSpec(memory_space=pltpu.VMEM),
        scratch_shapes=[
            pltpu.VMEM(inverse.shape, BF16),
            pltpu.VMEM((devices, 1, POINTS), F32),
            pltpu.SemaphoreType.DMA,
            pltpu.SemaphoreType.DMA,
            pltpu.SemaphoreType.DMA,
        ],
        compiler_params=pltpu.CompilerParams(collective_id=0, has_side_effects=True),
        cost_estimate=pl.CostEstimate(flops=2_000_000, bytes_accessed=2_100_000, transcendentals=0),
    )(resid, inverse)


def on_device(
    displacement, neighbours, micro_state, strain_loads, stiffness, expand_weight, contract_weight,
    batch_route, yield_flags, readout, external_force, coarse_inverse,
):
    devices = lax.axis_size("sub")
    disp = displacement[0]
    up = [(i, i + 1) for i in range(devices - 1)]
    down = [(i + 1, i) for i in range(devices - 1)]
    before = lax.ppermute(disp[:, POINTS - 1:], "sub", up)
    after = lax.ppermute(disp[:, :1], "sub", down)
    next_state, resid = micro_step(
        batch_route[0], yield_flags, disp, before, after, neighbours, strain_loads[0], readout, external_force,
        micro_state[0], stiffness[0], expand_weight[0], contract_weight[0],
    )
    coarse = coarse_step(resid, coarse_inverse[0], devices)
    return next_state[None], coarse


def solution(mesh):
    return jax.shard_map(
        on_device,
        mesh=mesh,
        in_specs=(
            P("variant", None, "sub"),
            P(None, "sub"),
            P("variant", "sub", None),
            P("variant", None, None),
            P("variant", None, None),
            P("variant", None, None),
            P("variant", None, None),
            P("variant", None, "sub"),
            P("variant", "sub"),
            P("variant", None),
            P("variant", "sub"),
            P("variant", "sub", None),
        ),
        out_specs=(P("variant", "sub", None), P("variant", "sub")),
        check_vma=False,
    )
```

time: 76.8 us -> 48.3 us (0.63)
  matrix products: 40.1 us -> 0 us
  Pallas kernels: 0 us -> 36.5 us
  blocking collectives: 22 us -> 0 us
  other arithmetic: 3.81 us -> 0 us
  local copies, waits for them, and re-layouts: 2.98 us -> 3.85 us
    dot_general x5 -> x0, matrix products: 40.1 us -> none  [the longest x1 21.2 us: plastic_update(): jnp.dot(hidden, contract_weight, preferred_element_type=jnp.float32)]
    pallas_call x0 -> x2, Pallas kernels: none -> 36.5 us  [the longest x1 21.1 us: coarse_step(): pl.pallas_call(functools.partial(coarse_kernel, devices), name='coarse',...]
    all_to_all x1 -> x0, blocking collectives: 22 us -> none  [sent_to_all(): return lax.all_to_all(copies, axis, split_axis=0, concat_axis=0, tiled=True)]
    unnamed x8 -> x9, local copies, waits for them, and re-layouts: 0.02 us -> 3.77 us
    convert_element_type x3 -> x0, other arithmetic: 1.46 us -> none  [the longest x1 0.78 us: on_device(): (jnp.repeat(alive_batch, BATCH) * yield_flags[0]).astype(jnp.float32)]
    gather x4 -> x0, local copies, waits for them, and re-layouts: 1.43 us -> none  [the longest x2 0.73 us: on_device(): upper_value = jnp.take(extended[0], neighbours[1], axis=1)]
    slice x1, local copies, waits for them, and re-layouts: 0.92 us -> 0.07 us  [on_device(): after = lax.ppermute(disp[:, :1], 'sub', down)]
    div x2 -> x0, other arithmetic: 0.78 us -> none  [on_device(): strain = (upper_value - lower_value) / spacing]
  transfers between devices with their start and end apart: 2 -> 2, of which waited for: 0 -> 0; matrix products, arithmetic and copies ran while one was open for 4% -> 3% of each run, Pallas kernels for 0% -> 0%
where the time goes in v1:
time: 48.3 us; the launch traced here: 48 us
  Pallas kernels  36.5 us (76%)
  starting transfers between devices  7.02 us (15%)
  local copies, waits for them, and re-layouts  3.85 us (8%)
  between operations  0.68 us (1%)
    pallas_call x1, Pallas kernels, coarse_step(): pl.pallas_call(functools.partial(coarse_kernel, devices), name='coarse',...  21.1 us
    pallas_call x1, Pallas kernels, micro_step(): pl.pallas_call(micro_kernel, name='micro', out_shape=(jax.ShapeDtypeStruc...  15.3 us
    ppermute x1, starting transfers between devices, on_device(): after = lax.ppermute(disp[:, :1], 'sub', down)  5.1 us
    unnamed x9, local copies, waits for them, and re-layouts  3.77 us
    ppermute x1, starting transfers between devices, on_device(): before = lax.ppermute(disp[:, POINTS - 1:], 'sub', up)  1.92 us
  transfers between devices with their start and end apart: 2, of which 0 were waited for; matrix products, arithmetic and copies ran while one was open for 3% of the time, Pallas kernels for 0%

profile of v1, /device:TPU:1, one launch (start us, length us, event | category | flops | bytes accessed | tf_op | source)
XLA Modules:
  0.0 48.0 jit_solution(10844349871275388848)
XLA Ops:
  0.6 0.7 %copy.19 = f32[1,6,128]{2,1,0:T(8,128)S(1)} copy(f32[1,6,128]{2,0,1:T(1,128)} %param.12) | data formatting | bytes 6144
  1.3 0.0 copy-start
  1.3 0.1 fusion
  1.4 5.1 %collective-permute-start.1 = (f32[6,1]{1,0:T(8,128)S(1)}, f32[6,1]{1,0:T(8,128)S(1)}, u32[]{:S(2)}, u32[]{:S(2)}) collective-permute-start(f32[6,1]{1,0:T(8,128)S(1)} %get-tuple-element.6), channel_id=1, source_target_pairs={{1,0},{2,1},{3,2},{4,3},{5,4},{6,5},{7,6},{8,7},{9,8},{10,9},{11,1... | collective-permute-start | bytes 80 | tf_op jit(solution)/shard_map/ppermute | solution.py:255
  6.5 1.9 %collective-permute-start = (f32[6,1]{1,0:T(8,128)S(1)}, f32[6,1]{1,0:T(8,128)S(1)}, u32[]{:S(2)}, u32[]{:S(2)}) collective-permute-start(f32[6,1]{1,0:T(8,128)S(1)} %get-tuple-element.7), channel_id=1, source_target_pairs={{0,1},{1,2},{2,3},{3,4},{4,5},{5,6},{6,7},{7,8},{8,9},{9,10},{10,1... | collective-permute-start | bytes 80 | tf_op jit(solution)/shard_map/ppermute | solution.py:254
  8.4 1.3 %copy.18 = f32[1,6,512]{2,1,0:T(8,128)} copy(f32[1,6,512]{2,0,1:T(1,128)} %param.15) | data formatting | bytes 24576
  9.7 0.0 collective-permute-done.1.after_ref
  9.7 0.0 copy-start.1
  9.7 0.0 collective-permute-done.before_ref
  9.7 0.0 copy-start.2
  9.8 0.0 copy-done
  9.8 0.6 %copy-done.1 = f32[6,1]{1,0:T(8,128)} copy-done((f32[6,1]{1,0:T(8,128)}, f32[6,1]{1,0:T(8,128)S(1)}, u32[]{:S(2)}) %copy-start.1) | copy-done | bytes 48
  10.3 0.0 copy-done.2
  10.3 15.3 %micro.1 = (bf16[3072,512]{1,0:T(8,128)(2,1)}, f32[1,128]{1,0:T(1,128)}) custom-call(s32[2,24]{1,0:T(2,128)} %bitcast.21, s32[1,3072]{1,0:T(1,128)} %flags_ref.1, f32[6,128]{1,0:T(8,128)} %bitcast.15, f32[6,1]{1,0:T(8,128)} %copy-done.2, f32[6,1]{1,0:T(8,128)} %copy-done.1, s32[2,128]{1,0:T(2,128)} %neigh_ref.1, f32[6,512]{1,0:T(8,128)} %bitcast.16, ...), custom_call_target="tpu_custom_call" | custom-call | flops 10000000000 | bytes 11000000 | tf_op jit(solution)/shard_map/micro/pallas_call | solution.py:167
  25.7 21.1 %coarse.1 = f32[1,128]{1,0:T(1,128)} custom-call(f32[1,128]{1,0:T(1,128)} %get-tuple-element.5.resid_ref, bf16[128,8192]{1,0:T(8,128)(2,1)} %bitcast.13), custom_call_target="tpu_custom_call" | custom-call | flops 2000000 | bytes 2100000 | tf_op jit(solution)/shard_map/coarse/pallas_call | solution.py:228
  46.8 1.2 %copy.21 = f32[1,128]{1,0:T(1,128)} copy(f32[1,128]{1,0:T(1,128)} %coarse.1) | data formatting | bytes 1024
Async XLA Ops:
  1.3 8.4 %copy-start = (f32[1,6,128]{2,1,0:T(8,128)}, f32[1,6,128]{2,1,0:T(8,128)S(1)}, u32[]{:S(2)}) copy-start(f32[1,6,128]{2,1,0:T(8,128)S(1)} %copy.19) | copy-start | bytes 9220
  1.4 8.3 %collective-permute-start.1 = (f32[6,1]{1,0:T(8,128)S(1)}, f32[6,1]{1,0:T(8,128)S(1)}, u32[]{:S(2)}, u32[]{:S(2)}) collective-permute-start(f32[6,1]{1,0:T(8,128)S(1)} %get-tuple-element.6), channel_id=1, source_target_pairs={{1,0},{2,1},{3,2},{4,3},{5,4},{6,5},{7,6},{8,7},{9,8},{10,9},{11,1... | collective-permute-start | bytes 80 | tf_op jit(solution)/shard_map/ppermute | solution.py:255
  6.5 3.2 %collective-permute-start = (f32[6,1]{1,0:T(8,128)S(1)}, f32[6,1]{1,0:T(8,128)S(1)}, u32[]{:S(2)}, u32[]{:S(2)}) collective-permute-start(f32[6,1]{1,0:T(8,128)S(1)} %get-tuple-element.7), channel_id=1, source_target_pairs={{0,1},{1,2},{2,3},{3,4},{4,5},{5,6},{6,7},{7,8},{8,9},{9,10},{10,1... | collective-permute-start | bytes 80 | tf_op jit(solution)/shard_map/ppermute | solution.py:254
  9.7 0.6 %copy-start.1 = (f32[6,1]{1,0:T(8,128)}, f32[6,1]{1,0:T(8,128)S(1)}, u32[]{:S(2)}) copy-start(f32[6,1]{1,0:T(8,128)S(1)} %collective-permute-done.1.after_ref) | copy-start | bytes 76
  9.7 0.6 %copy-start.2 = (f32[6,1]{1,0:T(8,128)}, f32[6,1]{1,0:T(8,128)S(1)}, u32[]{:S(2)}) copy-start(f32[6,1]{1,0:T(8,128)S(1)} %collective-permute-done.before_ref) | copy-start | bytes 76

commit v2 on v0

v2 whole, which is shorter than its diff:
```python
import functools

import jax
import jax.numpy as jnp
from jax import lax
from jax.experimental import pallas as pl
from jax.experimental.pallas import tpu as pltpu
from jax.sharding import PartitionSpec as P

BATCH = 128
RPP = 24
BATCHES = 24
SLOTS = 16
POINTS = 128
ROWS = 3072
MODES = 512
HIDDEN = 2048
STRAIN = 6
TILE = 384
TILES = ROWS // TILE
F32, BF16, I32 = jnp.float32, jnp.bfloat16, jnp.int32
MESH = pl.DeviceIdType.MESH


def mm(a, b, dims=((1,), (0,))):
    return lax.dot_general(a, b, (dims, ((), ())), preferred_element_type=F32)


def row_tile(rows):
    return jnp.concatenate(rows + [jnp.zeros((128 - len(rows), 128), rows[0].dtype)], axis=0)


def newton_kernel(
    devices,
    route_ref, flags_ref, disp_ref, neigh_ref, loads_ref, readout_ref, force_ref,
    micro_hbm, stiff_hbm, expand_hbm, contract_hbm, inverse_hbm,
    next_ref, coarse_ref,
    states, stiff, expand, contract, inverse, elastic, hidden, update, delta, weight_t, sums, halo, resid, blocks,
    in_sem, w_sem, halo_send, halo_recv, send_sem, recv_sem,
):
    def tile_rows(t):
        return pl.ds(t * TILE, TILE)

    me = lax.axis_index("sub") if devices > 1 else 0
    micro_in = [pltpu.make_async_copy(micro_hbm.at[tile_rows(t)], states.at[tile_rows(t)], in_sem.at[t]) for t in range(TILES)]
    stiff_in = pltpu.make_async_copy(stiff_hbm, stiff, w_sem.at[0])
    expand_in = pltpu.make_async_copy(expand_hbm, expand, w_sem.at[1])
    contract_in = pltpu.make_async_copy(contract_hbm, contract, w_sem.at[2])
    inverse_in = pltpu.make_async_copy(inverse_hbm, inverse, w_sem.at[3])
    stiff_in.start()
    for copy in micro_in:
        copy.start()
    expand_in.start()
    contract_in.start()
    inverse_in.start()
    if devices > 1:
        barrier = pltpu.get_barrier_semaphore()
        for d in range(1, devices):
            pl.semaphore_signal(barrier, inc=1, device_id={"sub": lax.rem(me + d, devices)}, device_id_type=MESH)

    alive = [(route_ref[0, b] >= 0).astype(I32) for b in range(BATCHES)]
    ranks, upto, seen = [], [], jnp.int32(0)
    for b in range(1, BATCHES - 1):
        ranks.append(seen)
        seen = seen + alive[b]
        upto.append(seen)

    def inner(rank):
        passed = jnp.int32(1)
        for total in upto:
            passed = passed + (total <= rank).astype(I32)
        return jnp.minimum(passed, BATCHES - 2)

    first, last = alive[0] > 0, alive[-1] > 0
    held = [inner(j) for j in range(SLOTS)]
    held[15] = jnp.where(last, BATCHES - 1, jnp.where(first, held[14], held[15]))
    held[14] = jnp.where(first, 0, held[14])
    slots = [jnp.int32(14)] + [
        jnp.minimum(jnp.where(rank == 14, jnp.where(first, 15, 14), rank), SLOTS - 1) for rank in ranks
    ] + [jnp.int32(15)]

    weight_t[...] = row_tile([flags_ref[0:1, b * BATCH:(b + 1) * BATCH] for b in range(BATCHES)]).astype(F32).T

    here = lax.broadcasted_iota(I32, (1, POINTS), 1)
    low_i, high_i = neigh_ref[0:1, :], neigh_ref[1:2, :]
    spacing = (high_i - low_i).astype(F32)

    def shift_of(before, after):
        rows = []
        for k in range(STRAIN):
            disp = disp_ref[k]
            prev = jnp.where(here == 0, before(k), pltpu.roll(disp, 1, 1))
            follow = jnp.where(here == POINTS - 1, after(k), pltpu.roll(disp, POINTS - 1, 1))
            lower = jnp.where(low_i == here, prev, disp)
            upper = jnp.where(high_i == here + 2, follow, disp)
            rows.append((upper - lower) / spacing)
        return row_tile(rows).T

    def load_of(strain_t, part):
        total = strain_t[part, 0:1] * loads_ref[0]
        for k in range(1, STRAIN):
            total = total + strain_t[part, k:k + 1] * loads_ref[k]
        return total

    delta[...] = load_of(shift_of(lambda k: 0.0, lambda k: 0.0), slice(0, POINTS))

    def elastic_of(t, batches):
        shift = jnp.concatenate(
            [jnp.broadcast_to(delta[p:p + 1, :], (RPP, MODES)) for p in range(t * 16, t * 16 + 16)], axis=0
        )
        lo, hi = batches[0] * BATCH - t * TILE, (batches[-1] + 1) * BATCH - t * TILE
        trial = (states[tile_rows(t), :][lo:hi].astype(F32) + shift[lo:hi]).astype(BF16)
        rows = mm(trial, stiff[...]).astype(BF16)
        for j, b in enumerate(batches):
            elastic[b] = rows[j * BATCH:(j + 1) * BATCH]

    stiff_in.wait()
    for t in range(TILES):
        micro_in[t].wait()
        elastic_of(t, [b for b in range(t * 3, t * 3 + 3) if 0 < b < BATCHES - 1])

    def plastic(group):
        x = jnp.concatenate([elastic[held[j]] for j in group], axis=0)
        length = len(group) * BATCH
        for n in range(4):
            cols = slice(n * 512, (n + 1) * 512)
            a = mm(x, expand[:, cols])
            hidden[0:length, cols] = (a * (0.5 + 0.5 * jnp.tanh(0.5 * a))).astype(BF16)
        out = mm(hidden[0:length, :], contract[...]).astype(BF16)
        for i, j in enumerate(group):
            update[j] = out[i * BATCH:(i + 1) * BATCH]

    expand_in.wait()
    contract_in.wait()
    plastic([0, 1, 2, 3])
    plastic([4, 5, 6, 7])
    halo_copies = []
    if devices > 1:
        pl.semaphore_wait(barrier, devices - 1)
        for side, step in ((0, 1), (1, devices - 1)):
            copy = pltpu.make_async_remote_copy(
                src_ref=disp_ref, dst_ref=halo.at[side], send_sem=halo_send.at[side], recv_sem=halo_recv.at[side],
                device_id={"sub": lax.rem(me + step, devices)}, device_id_type=MESH,
            )
            copy.start()
            halo_copies.append(copy)
    plastic([8, 9, 10, 11])
    for copy in halo_copies:
        copy.wait()

    def before(k):
        return jnp.where(me == 0, 0.0, pltpu.roll(halo[0, k], 1, 1))

    def after(k):
        return jnp.where(me == devices - 1, 0.0, pltpu.roll(halo[1, k], POINTS - 1, 1))

    strain_t = shift_of(before, after)
    delta[0:8, :] = load_of(strain_t, slice(0, 8))
    delta[POINTS - 8:, :] = load_of(strain_t, slice(POINTS - 8, POINTS))
    elastic_of(0, [0])
    elastic_of(TILES - 1, [BATCHES - 1])
    plastic([12, 13, 14, 15])

    members = (
        lax.broadcasted_iota(I32, (16, TILE), 1) // RPP == lax.broadcasted_iota(I32, (16, TILE), 0)
    ).astype(BF16)
    for t in range(TILES):
        for b in range(t * 3, t * 3 + 3):
            weight = weight_t[:, b:b + 1] * alive[b].astype(F32)
            rows = elastic[b].astype(F32) + weight * update[slots[b]].astype(F32)
            next_ref[b * BATCH:(b + 1) * BATCH, :] = rows.astype(BF16)
        sums[t * 16:(t + 1) * 16, :] = mm(members, next_ref[tile_rows(t), :])
    weighed = sums[...] * readout_ref[...].astype(F32)
    lanes = weighed[:, 0:128] + weighed[:, 128:256] + weighed[:, 256:384] + weighed[:, 384:512]
    mean = jnp.sum(lanes.T, axis=0, keepdims=True) / RPP
    resid[...] = (force_ref[...] - mean).astype(BF16).astype(F32)

    inverse_in.wait()
    if devices == 1:
        coarse_ref[...] = resid[...]
        return
    for d in range(1, devices):
        pltpu.make_async_remote_copy(
            src_ref=resid, dst_ref=blocks.at[me], send_sem=send_sem, recv_sem=recv_sem,
            device_id={"sub": lax.rem(me + d, devices)}, device_id_type=MESH,
        ).start()
    blocks[me] = resid[...]
    others = blocks.at[pl.ds(0, devices - 1)]
    pltpu.make_async_copy(others, others, recv_sem).wait()
    acc = None
    for s in range(devices):
        part = inverse[:, s * POINTS:(s + 1) * POINTS].astype(F32) * blocks[s]
        acc = part if acc is None else acc + part
    coarse_ref[...] = jnp.sum(acc.T, axis=0, keepdims=True)
    pltpu.make_async_copy(others, others, send_sem).wait()


def newton_step(devices, *operands):
    smem = pl.BlockSpec(memory_space=pltpu.SMEM)
    vmem = pl.BlockSpec(memory_space=pltpu.VMEM)
    hbm = pl.BlockSpec(memory_space=pl.ANY)
    params = pltpu.CompilerParams(collective_id=0, has_side_effects=True) if devices > 1 else None
    return pl.pallas_call(
        functools.partial(newton_kernel, devices),
        name="newton",
        out_shape=(jax.ShapeDtypeStruct((ROWS, MODES), BF16), jax.ShapeDtypeStruct((1, POINTS), F32)),
        in_specs=[smem] + [vmem] * 6 + [hbm] * 5,
        out_specs=(vmem, vmem),
        scratch_shapes=[
            pltpu.VMEM((ROWS, MODES), BF16),
            pltpu.VMEM((MODES, MODES), BF16),
            pltpu.VMEM((MODES, HIDDEN), BF16),
            pltpu.VMEM((HIDDEN, MODES), BF16),
            pltpu.VMEM((POINTS, 64 * POINTS), BF16),
            pltpu.VMEM((BATCHES, BATCH, MODES), BF16),
            pltpu.VMEM((4 * BATCH, HIDDEN), BF16),
            pltpu.VMEM((SLOTS, BATCH, MODES), BF16),
            pltpu.VMEM((POINTS, MODES), F32),
            pltpu.VMEM((128, 128), F32),
            pltpu.VMEM((POINTS, MODES), F32),
            pltpu.VMEM((2, STRAIN, 1, POINTS), F32),
            pltpu.VMEM((1, POINTS), F32),
            pltpu.VMEM((64, 1, POINTS), F32),
            pltpu.SemaphoreType.DMA((TILES,)),
            pltpu.SemaphoreType.DMA((4,)),
            pltpu.SemaphoreType.DMA((2,)),
            pltpu.SemaphoreType.DMA((2,)),
            pltpu.SemaphoreType.DMA,
            pltpu.SemaphoreType.DMA,
        ],
        compiler_params=params,
    )(*operands)


def on_device(
    displacement, neighbours, micro_state, strain_loads, stiffness, expand_weight, contract_weight,
    batch_route, yield_flags, readout, external_force, coarse_inverse,
):
    next_state, coarse = newton_step(
        lax.axis_size("sub"),
        batch_route[0], yield_flags, displacement.transpose(1, 0, 2), neighbours, strain_loads.transpose(1, 0, 2),
        readout, external_force, micro_state[0], stiffness[0], expand_weight[0], contract_weight[0], coarse_inverse[0],
    )
    return next_state[None], coarse


def solution(mesh):
    return jax.shard_map(
        on_device,
        mesh=mesh,
        in_specs=(
            P("variant", None, "sub"),
            P(None, "sub"),
            P("variant", "sub", None),
            P("variant", None, None),
            P("variant", None, None),
            P("variant", None, None),
            P("variant", None, None),
            P("variant", None, "sub"),
            P("variant", "sub"),
            P("variant", None),
            P("variant", "sub"),
            P("variant", "sub", None),
        ),
        out_specs=(P("variant", "sub", None), P("variant", "sub")),
        check_vma=False,
    )
```

time: 76.8 us -> 36.8 us (0.48)
  matrix products: 40.1 us -> 0 us
  Pallas kernels: 0 us -> 31.7 us
  blocking collectives: 22 us -> 0 us
  starting transfers between devices: 6.84 us -> 0 us
  other arithmetic: 3.81 us -> 0 us
  local copies, waits for them, and re-layouts: 2.98 us -> 4.27 us
    dot_general x5 -> x0, matrix products: 40.1 us -> none  [the longest x1 21.2 us: plastic_update(): jnp.dot(hidden, contract_weight, preferred_element_type=jnp.float32)]
    pallas_call x0 -> x1, Pallas kernels: none -> 31.7 us  [newton_step(): pl.pallas_call(functools.partial(newton_kernel, devices), name='newton',...]
    all_to_all x1 -> x0, blocking collectives: 22 us -> none  [sent_to_all(): return lax.all_to_all(copies, axis, split_axis=0, concat_axis=0, tiled=True)]
    ppermute x2 -> x0, starting transfers between devices: 6.84 us -> none  [the longest x1 4.92 us: extended_2(): before = lax.ppermute(last, axis, up)]
    unnamed x8 -> x4, local copies, waits for them, and re-layouts: 0.02 us -> 4.27 us
    convert_element_type x3 -> x0, other arithmetic: 1.46 us -> none  [the longest x1 0.78 us: on_device(): (jnp.repeat(alive_batch, BATCH) * yield_flags[0]).astype(jnp.float32)]
    gather x4 -> x0, local copies, waits for them, and re-layouts: 1.43 us -> none  [the longest x2 0.73 us: on_device(): upper_value = jnp.take(extended[0], neighbours[1], axis=1)]
    slice x1 -> x0, local copies, waits for them, and re-layouts: 0.92 us -> none  [extended_2(): last = lax.slice_in_dim(x, length - width, length, axis=dim)]
  transfers between devices with their start and end apart: 2 -> 0, of which waited for: 0 -> 0; matrix products, arithmetic and copies ran while one was open for 4% -> 0% of each run, Pallas kernels for 0% -> 0%
where the time goes in v2:
time: 36.8 us; the launch traced here: 36.7 us
  Pallas kernels  31.7 us (86%)
  local copies, waits for them, and re-layouts  4.27 us (12%)
  between operations  0.65 us (2%)
    pallas_call x1, Pallas kernels, newton_step(): pl.pallas_call(functools.partial(newton_kernel, devices), name='newton',...  31.7 us
    unnamed x4, local copies, waits for them, and re-layouts  4.27 us

profile of v2, /device:TPU:1, one launch (start us, length us, event | category | flops | bytes accessed | tf_op | source)
XLA Modules:
  0.0 36.7 jit_solution(17572203349865864973)
XLA Ops:
  0.6 31.7 %newton.1 = (bf16[3072,512]{1,0:T(8,128)(2,1)}, f32[1,128]{1,0:T(1,128)}) custom-call(s32[2,24]{1,0:T(2,128)} %bitcast.17, s32[1,3072]{1,0:T(1,128)} %flags_ref.1, f32[6,1,128]{2,1,0:T(1,128)} %bitcast.16, s32[2,128]{1,0:T(2,128)} %neigh_ref.1, f32[6,1,512]{2,1,0:T(1,128)} %bitcast.15, bf16[1,512]{1,0:T(2,128)(2,1)} %readout_ref.1, f32[1,128]{1,0:T(1,128)} %force_ref.1, ...), custom_call_target="tpu_custom_call" | custom-call | tf_op jit(solution)/shard_map/newton/pallas_call | solution.py:203
  32.4 0.0 copy-start
  32.4 3.8 %copy.16 = bf16[1,3072,512]{2,1,0:T(8,128)(2,1)} copy(bf16[1,3072,512]{2,1,0:T(8,128)(2,1)} %bitcast.9) | data formatting | bytes 6291456
  36.1 0.0 copy-done
  36.2 0.5 %copy.17 = f32[1,128]{1,0:T(1,128)} copy(f32[1,128]{1,0:T(1,128)S(1)} %copy-done) | data formatting | bytes 1024
Async XLA Ops:
  32.4 3.8 %copy-start = (f32[1,128]{1,0:T(1,128)S(1)}, f32[1,128]{1,0:T(1,128)}, u32[]{:S(2)}) copy-start(f32[1,128]{1,0:T(1,128)} %get-tuple-element.9) | copy-start | bytes 1540

commit v3 on v2

--- a/solution.py
+++ b/solution.py
@@ -10,6 +10,8 @@
 BATCH = 128
 RPP = 24
 BATCHES = 24
+LIMIT = 58 << 20
+PIECE = 32
 SLOTS = 16
 POINTS = 128
 ROWS = 3072
@@ -32,11 +34,12 @@
 
 def newton_kernel(
     devices,
-    route_ref, flags_ref, disp_ref, neigh_ref, loads_ref, readout_ref, force_ref,
+    route_hbm, flags_hbm, disp_hbm, neigh_hbm, loads_hbm, readout_hbm, force_hbm,
     micro_hbm, stiff_hbm, expand_hbm, contract_hbm, inverse_hbm,
     next_ref, coarse_ref,
+    route_ref, flags_ref, disp_ref, neigh_ref, loads_ref, readout_ref, force_ref,
     states, stiff, expand, contract, inverse, elastic, hidden, update, delta, weight_t, sums, halo, resid, blocks,
-    in_sem, w_sem, halo_send, halo_recv, send_sem, recv_sem,
+    small_sem, in_sem, w_sem, halo_send, halo_recv, send_sem, recv_sem,
 ):
     def tile_rows(t):
         return pl.ds(t * TILE, TILE)
@@ -47,40 +50,29 @@
     expand_in = pltpu.make_async_copy(expand_hbm, expand, w_sem.at[1])
     contract_in = pltpu.make_async_copy(contract_hbm, contract, w_sem.at[2])
     inverse_in = pltpu.make_async_copy(inverse_hbm, inverse, w_sem.at[3])
+    small_in = [
+        pltpu.make_async_copy(src, dst, small_sem.at[i])
+        for i, (src, dst) in enumerate((
+            (disp_hbm, disp_ref), (neigh_hbm, neigh_ref), (loads_hbm, loads_ref),
+            (route_hbm, route_ref), (flags_hbm, flags_ref), (readout_hbm, readout_ref), (force_hbm, force_ref),
+        ))
+    ]
+    for copy in small_in[:3]:
+        copy.start()
     stiff_in.start()
-    for copy in micro_in:
-        copy.start()
-    expand_in.start()
-    contract_in.start()
-    inverse_in.start()
+    for copy in micro_in[:2]:
+        copy.start()
+    for copy in small_in[3:]:
+        copy.start()
+    for copy in micro_in[2:]:
+        copy.start()
     if devices > 1:
         barrier = pltpu.get_barrier_semaphore()
         for d in range(1, devices):
             pl.semaphore_signal(barrier, inc=1, device_id={"sub": lax.rem(me + d, devices)}, device_id_type=MESH)
 
-    alive = [(route_ref[0, b] >= 0).astype(I32) for b in range(BATCHES)]
-    ranks, upto, seen = [], [], jnp.int32(0)
-    for b in range(1, BATCHES - 1):
-        ranks.append(seen)
-        seen = seen + alive[b]
-        upto.append(seen)
-
-    def inner(rank):
-        passed = jnp.int32(1)
-        for total in upto:
-            passed = passed + (total <= rank).astype(I32)
-        return jnp.minimum(passed, BATCHES - 2)
-
-    first, last = alive[0] > 0, alive[-1] > 0
-    held = [inner(j) for j in range(SLOTS)]
-    held[15] = jnp.where(last, BATCHES - 1, jnp.where(first, held[14], held[15]))
-    held[14] = jnp.where(first, 0, held[14])
-    slots = [jnp.int32(14)] + [
-        jnp.minimum(jnp.where(rank == 14, jnp.where(first, 15, 14), rank), SLOTS - 1) for rank in ranks
-    ] + [jnp.int32(15)]
-
-    weight_t[...] = row_tile([flags_ref[0:1, b * BATCH:(b + 1) * BATCH] for b in range(BATCHES)]).astype(F32).T
-
+    for copy in small_in[:3]:
+        copy.wait()
     here = lax.broadcasted_iota(I32, (1, POINTS), 1)
     low_i, high_i = neigh_ref[0:1, :], neigh_ref[1:2, :]
     spacing = (high_i - low_i).astype(F32)
@@ -114,26 +106,76 @@
         for j, b in enumerate(batches):
             elastic[b] = rows[j * BATCH:(j + 1) * BATCH]
 
-    stiff_in.wait()
-    for t in range(TILES):
+    def elastic_tile(t):
         micro_in[t].wait()
         elastic_of(t, [b for b in range(t * 3, t * 3 + 3) if 0 < b < BATCHES - 1])
 
-    def plastic(group):
+    stiff_in.wait()
+    for t in range(3):
+        elastic_tile(t)
+    expand_in.start()
+    contract_in.start()
+    for copy in small_in[3:]:
+        copy.wait()
+    alive = [(route_ref[0, b] >= 0).astype(I32) for b in range(BATCHES)]
+    ranks, upto, seen = [], [], jnp.int32(0)
+    for b in range(1, BATCHES - 1):
+        ranks.append(seen)
+        seen = seen + alive[b]
+        upto.append(seen)
+
+    def inner(rank):
+        passed = jnp.int32(1)
+        for total in upto:
+            passed = passed + (total <= rank).astype(I32)
+        return jnp.minimum(passed, BATCHES - 2)
+
+    first, last = alive[0] > 0, alive[-1] > 0
+    held = [inner(j) for j in range(SLOTS)]
+    held[15] = jnp.where(last, BATCHES - 1, jnp.where(first, held[14], held[15]))
+    held[14] = jnp.where(first, 0, held[14])
+    slots = [jnp.int32(14)] + [
+        jnp.minimum(jnp.where(rank == 14, jnp.where(first, 15, 14), rank), SLOTS - 1) for rank in ranks
+    ] + [jnp.int32(15)]
+
+    weight_t[...] = row_tile(
+        [(flags_ref[0:1, b * BATCH:(b + 1) * BATCH] * alive[b]).astype(F32) for b in range(BATCHES)]
+    ).T
+
+    for t in range(3, TILES):
+        elastic_tile(t)
+    inverse_in.start()
+
+    def plastic(group, between=()):
         x = jnp.concatenate([elastic[held[j]] for j in group], axis=0)
         length = len(group) * BATCH
         for n in range(4):
             cols = slice(n * 512, (n + 1) * 512)
             a = mm(x, expand[:, cols])
             hidden[0:length, cols] = (a * (0.5 + 0.5 * jnp.tanh(0.5 * a))).astype(BF16)
+            if n < len(between):
+                between[n]()
         out = mm(hidden[0:length, :], contract[...]).astype(BF16)
         for i, j in enumerate(group):
             update[j] = out[i * BATCH:(i + 1) * BATCH]
 
+    members = (
+        lax.broadcasted_iota(I32, (16, TILE), 1) // RPP == lax.broadcasted_iota(I32, (16, TILE), 0)
+    ).astype(BF16)
+
+    def finish(b):
+        for r in range(0, BATCH, PIECE):
+            part = slice(r, r + PIECE)
+            rows = elastic[b, part].astype(F32) + weight_t[part, b:b + 1] * update[slots[b], part].astype(F32)
+            next_ref[b * BATCH + r:b * BATCH + r + PIECE, :] = rows.astype(BF16)
+
+    def sum_up(t):
+        sums[t * 16:(t + 1) * 16, :] = mm(members, next_ref[tile_rows(t), :])
+
     expand_in.wait()
     contract_in.wait()
     plastic([0, 1, 2, 3])
-    plastic([4, 5, 6, 7])
+    plastic([4, 5, 6, 7], [functools.partial(finish, b) for b in (1, 2, 3, 4)])
     halo_copies = []
     if devices > 1:
         pl.semaphore_wait(barrier, devices - 1)
@@ -144,7 +186,7 @@
             )
             copy.start()
             halo_copies.append(copy)
-    plastic([8, 9, 10, 11])
+    plastic([8, 9, 10, 11], [functools.partial(finish, b) for b in (5, 6, 7, 8)])
     for copy in halo_copies:
         copy.wait()
 
@@ -159,17 +201,14 @@
     delta[POINTS - 8:, :] = load_of(strain_t, slice(POINTS - 8, POINTS))
     elastic_of(0, [0])
     elastic_of(TILES - 1, [BATCHES - 1])
-    plastic([12, 13, 14, 15])
-
-    members = (
-        lax.broadcasted_iota(I32, (16, TILE), 1) // RPP == lax.broadcasted_iota(I32, (16, TILE), 0)
-    ).astype(BF16)
-    for t in range(TILES):
+    plastic([12, 13, 14, 15], [functools.partial(finish, b) for b in (9, 10, 11, 12)])
+    for t in (1, 2, 3):
+        sum_up(t)
+    for t in (4, 5, 6, 7, 0):
         for b in range(t * 3, t * 3 + 3):
-            weight = weight_t[:, b:b + 1] * alive[b].astype(F32)
-            rows = elastic[b].astype(F32) + weight * update[slots[b]].astype(F32)
-            next_ref[b * BATCH:(b + 1) * BATCH, :] = rows.astype(BF16)
-        sums[t * 16:(t + 1) * 16, :] = mm(members, next_ref[tile_rows(t), :])
+            if not 0 < b < 13:
+                finish(b)
+        sum_up(t)
     weighed = sums[...] * readout_ref[...].astype(F32)
     lanes = weighed[:, 0:128] + weighed[:, 128:256] + weighed[:, 256:384] + weighed[:, 384:512]
     mean = jnp.sum(lanes.T, axis=0, keepdims=True) / RPP
@@ -179,34 +218,78 @@
     if devices == 1:
         coarse_ref[...] = resid[...]
         return
-    for d in range(1, devices):
+    blocks[me] = resid[...]
+    plane, depth, core = me // 16, lax.rem(me // 2, 8), lax.rem(me, 2)
+    for dx, dz, dc in sorted(
+        ((dx, dz, dc) for dx in range(4) for dz in range(8) for dc in range(2) if dx or dz or dc),
+        key=lambda step: -min(step[0], 4 - step[0]) - min(step[1], 8 - step[1]),
+    ):
+        peer = lax.rem(plane + dx, 4) * 16 + lax.rem(depth + dz, 8) * 2 + lax.rem(core + dc, 2)
         pltpu.make_async_remote_copy(
-            src_ref=resid, dst_ref=blocks.at[me], send_sem=send_sem, recv_sem=recv_sem,
-            device_id={"sub": lax.rem(me + d, devices)}, device_id_type=MESH,
+            src_ref=resid, dst_ref=blocks.at[me], send_sem=send_sem, recv_sem=recv_sem.at[plane],
+            device_id={"sub": peer}, device_id_type=MESH,
         ).start()
-    blocks[me] = resid[...]
+    acc = None
+    for dx in (0, 1, 3, 2):
+        near = lax.rem(plane + dx, 4)
+        arrived = blocks.at[pl.ds(0, 15 if dx == 0 else 16)]
+        pltpu.make_async_copy(arrived, arrived, recv_sem.at[near]).wait()
+        for s in range(16):
+            column = pl.multiple_of((near * 16 + s) * POINTS, POINTS)
+            part = inverse[:, pl.ds(column, POINTS)].astype(F32) * blocks[near * 16 + s]
+            acc = part if acc is None else acc + part
+    coarse_ref[...] = jnp.sum(acc.T, axis=0, keepdims=True)
     others = blocks.at[pl.ds(0, devices - 1)]
-    pltpu.make_async_copy(others, others, recv_sem).wait()
-    acc = None
-    for s in range(devices):
-        part = inverse[:, s * POINTS:(s + 1) * POINTS].astype(F32) * blocks[s]
-        acc = part if acc is None else acc + part
-    coarse_ref[...] = jnp.sum(acc.T, axis=0, keepdims=True)
     pltpu.make_async_copy(others, others, send_sem).wait()
 
 
+def write_kernel(next_vmem, coarse_vmem, next_hbm, coarse_hbm, sem):
+    part = ROWS // 4
+    copies = [pltpu.make_async_copy(coarse_vmem, coarse_hbm, sem.at[4])]
+    for i in range(4):
+        rows = pl.ds(i * part, part)
+        copies.append(pltpu.make_async_copy(next_vmem.at[rows], next_hbm.at[rows], sem.at[i]))
+    for copy in copies:
+        copy.start()
+    for copy in copies:
+        copy.wait()
+
+
+def write_out(next_state, coarse):
+    place = pl.BlockSpec(memory_space=pl.ANY)
+    return pl.pallas_call(
+        write_kernel,
+        name="write",
+        out_shape=(pltpu.HBM((ROWS, MODES), BF16), pltpu.HBM((1, POINTS), F32)),
+        in_specs=[pl.BlockSpec(memory_space=pltpu.VMEM)] * 2,
+        out_specs=(pl.BlockSpec(memory_space=pltpu.HBM),) * 2,
+        scratch_shapes=[pltpu.SemaphoreType.DMA((5,))],
+        compiler_params=pltpu.CompilerParams(vmem_limit_bytes=1 << 20),
+    )(next_state, coarse)
+
+
 def newton_step(devices, *operands):
-    smem = pl.BlockSpec(memory_space=pltpu.SMEM)
     vmem = pl.BlockSpec(memory_space=pltpu.VMEM)
-    hbm = pl.BlockSpec(memory_space=pl.ANY)
-    params = pltpu.CompilerParams(collective_id=0, has_side_effects=True) if devices > 1 else None
+    hbm = pl.BlockSpec(memory_space=pltpu.HBM)
+    params = (
+        pltpu.CompilerParams(collective_id=0, has_side_effects=True, vmem_limit_bytes=LIMIT)
+        if devices > 1
+        else pltpu.CompilerParams(vmem_limit_bytes=LIMIT)
+    )
     return pl.pallas_call(
         functools.partial(newton_kernel, devices),
         name="newton",
-        out_shape=(jax.ShapeDtypeStruct((ROWS, MODES), BF16), jax.ShapeDtypeStruct((1, POINTS), F32)),
-        in_specs=[smem] + [vmem] * 6 + [hbm] * 5,
+        out_shape=(pltpu.VMEM((ROWS, MODES), BF16), pltpu.VMEM((1, POINTS), F32)),
+        in_specs=[hbm] * 12,
         out_specs=(vmem, vmem),
         scratch_shapes=[
+            pltpu.SMEM((2, BATCHES), I32),
+            pltpu.VMEM((1, ROWS), I32),
+            pltpu.VMEM((STRAIN, 1, POINTS), F32),
+            pltpu.VMEM((2, POINTS), I32),
+            pltpu.VMEM((STRAIN, 1, MODES), F32),
+            pltpu.VMEM((1, MODES), BF16),
+            pltpu.VMEM((1, POINTS), F32),
             pltpu.VMEM((ROWS, MODES), BF16),
             pltpu.VMEM((MODES, MODES), BF16),
             pltpu.VMEM((MODES, HIDDEN), BF16),
@@ -221,12 +304,13 @@
             pltpu.VMEM((2, STRAIN, 1, POINTS), F32),
             pltpu.VMEM((1, POINTS), F32),
             pltpu.VMEM((64, 1, POINTS), F32),
+            pltpu.SemaphoreType.DMA((7,)),
             pltpu.SemaphoreType.DMA((TILES,)),
             pltpu.SemaphoreType.DMA((4,)),
             pltpu.SemaphoreType.DMA((2,)),
             pltpu.SemaphoreType.DMA((2,)),
             pltpu.SemaphoreType.DMA,
-            pltpu.SemaphoreType.DMA,
+            pltpu.SemaphoreType.DMA((4,)),
         ],
         compiler_params=params,
     )(*operands)
@@ -241,6 +325,7 @@
         batch_route[0], yield_flags, displacement.transpose(1, 0, 2), neighbours, strain_loads.transpose(1, 0, 2),
         readout, external_force, micro_state[0], stiffness[0], expand_weight[0], contract_weight[0], coarse_inverse[0],
     )
+    next_state, coarse = write_out(next_state, coarse)
     return next_state[None], coarse
 
 

time: 36.8 us -> 31.6 us (0.86)
  local copies, waits for them, and re-layouts: 4.27 us -> 0 us
  Pallas kernels: 31.7 us -> 30.9 us
    unnamed x4 -> x0, local copies, waits for them, and re-layouts: 4.27 us -> none
    pallas_call x1, Pallas kernels: 31.7 us -> 29.2 us  [newton_step(): pl.pallas_call(functools.partial(newton_kernel, devices), name='newton',...]
    pallas_call x0 -> x1, Pallas kernels: none -> 1.7 us  [write_out(): pl.pallas_call(write_kernel, name='write', out_shape=(pltpu.HBM((ROWS, MO...]
where the time goes in v3:
time: 31.6 us; the launch traced here: 31.5 us
  Pallas kernels  30.9 us (98%)
  between operations  0.64 us (2%)
    pallas_call x1, Pallas kernels, newton_step(): pl.pallas_call(functools.partial(newton_kernel, devices), name='newton',...  29.2 us
    pallas_call x1, Pallas kernels, write_out(): pl.pallas_call(write_kernel, name='write', out_shape=(pltpu.HBM((ROWS, MO...  1.7 us

profile of v3, /device:TPU:1, one launch (start us, length us, event | category | flops | bytes accessed | tf_op | source)
XLA Modules:
  0.0 31.5 jit_solution(901795148182204685)
XLA Ops:
  0.6 29.2 %newton.1 = (bf16[3072,512]{1,0:T(8,128)(2,1)S(1)}, f32[1,128]{1,0:T(1,128)S(1)}) custom-call(s32[2,24]{1,0:T(2,128)} %bitcast.16, s32[1,3072]{1,0:T(1,128)} %flags_hbm.1, f32[6,1,128]{2,1,0:T(1,128)} %bitcast.15, s32[2,128]{1,0:T(2,128)} %neigh_hbm.1, f32[6,1,512]{2,1,0:T(1,128)} %bitcast.14, bf16[1,512]{1,0:T(2,128)(2,1)} %readout_hbm.1, ...), custom_call_target="tpu_custom_call" | custom-call | tf_op jit(solution)/shard_map/newton/pallas_call | solution.py:279
  29.8 1.7 %write.1 = (bf16[3072,512]{1,0:T(8,128)(2,1)}, f32[1,128]{1,0:T(1,128)}) custom-call(bf16[3072,512]{1,0:T(8,128)(2,1)S(1)} %get-tuple-element.6.next_vmem, f32[1,128]{1,0:T(1,128)S(1)} %get-tuple-element.7.coarse_vmem), custom_call_target="tpu_custom_call" | custom-call | tf_op jit(solution)/shard_map/write/pallas_call | solution.py:260

commit v4 on v3

--- a/solution.py
+++ b/solution.py
@@ -11,7 +11,8 @@
 RPP = 24
 BATCHES = 24
 LIMIT = 58 << 20
-PIECE = 32
+RB = 512
+NB = 512
 SLOTS = 16
 POINTS = 128
 ROWS = 3072
@@ -66,6 +67,8 @@
         copy.start()
     for copy in micro_in[2:]:
         copy.start()
+    expand_in.start()
+    contract_in.start()
     if devices > 1:
         barrier = pltpu.get_barrier_semaphore()
         for d in range(1, devices):
@@ -106,15 +109,16 @@
         for j, b in enumerate(batches):
             elastic[b] = rows[j * BATCH:(j + 1) * BATCH]
 
-    def elastic_tile(t):
+    def elastic_tile(t, wait=True):
+        if wait:
+            micro_in[t].wait()
+        elastic_of(t, [b for b in range(t * 3, t * 3 + 3) if 0 < b < BATCHES - 1])
+
+    stiff_in.wait()
+    for t in range(2):
+        elastic_tile(t)
+    for t in range(2, TILES):
         micro_in[t].wait()
-        elastic_of(t, [b for b in range(t * 3, t * 3 + 3) if 0 < b < BATCHES - 1])
-
-    stiff_in.wait()
-    for t in range(3):
-        elastic_tile(t)
-    expand_in.start()
-    contract_in.start()
     for copy in small_in[3:]:
         copy.wait()
     alive = [(route_ref[0, b] >= 0).astype(I32) for b in range(BATCHES)]
@@ -125,8 +129,8 @@
         upto.append(seen)
 
     def inner(rank):
-        passed = jnp.int32(1)
-        for total in upto:
+        passed = jnp.int32(1 + rank)
+        for total in upto[rank:]:
             passed = passed + (total <= rank).astype(I32)
         return jnp.minimum(passed, BATCHES - 2)
 
@@ -142,32 +146,34 @@
         [(flags_ref[0:1, b * BATCH:(b + 1) * BATCH] * alive[b]).astype(F32) for b in range(BATCHES)]
     ).T
 
-    for t in range(3, TILES):
-        elastic_tile(t)
+    for t in range(2, TILES):
+        elastic_tile(t, False)
     inverse_in.start()
 
     def plastic(group, between=()):
         x = jnp.concatenate([elastic[held[j]] for j in group], axis=0)
         length = len(group) * BATCH
-        for n in range(4):
-            cols = slice(n * 512, (n + 1) * 512)
-            a = mm(x, expand[:, cols])
-            hidden[0:length, cols] = (a * (0.5 + 0.5 * jnp.tanh(0.5 * a))).astype(BF16)
-            if n < len(between):
-                between[n]()
-        out = mm(hidden[0:length, :], contract[...]).astype(BF16)
-        for i, j in enumerate(group):
-            update[j] = out[i * BATCH:(i + 1) * BATCH]
+        for n in range(HIDDEN // NB):
+            cols = slice(n * NB, (n + 1) * NB)
+            for r in range(0, length, RB):
+                a = mm(x[r:r + RB], expand[:, cols])
+                hidden[r:r + RB, cols] = (a * (0.5 + 0.5 * jnp.tanh(0.5 * a))).astype(BF16)
+            for piece in between[n * NB // 512:(n + 1) * NB // 512]:
+                piece()
+        for r in range(0, length, RB):
+            out = mm(hidden[r:r + RB, :], contract[...]).astype(BF16)
+            for i in range(RB // BATCH):
+                update[group[r // BATCH + i]] = out[i * BATCH:(i + 1) * BATCH]
 
     members = (
         lax.broadcasted_iota(I32, (16, TILE), 1) // RPP == lax.broadcasted_iota(I32, (16, TILE), 0)
     ).astype(BF16)
 
     def finish(b):
-        for r in range(0, BATCH, PIECE):
-            part = slice(r, r + PIECE)
-            rows = elastic[b, part].astype(F32) + weight_t[part, b:b + 1] * update[slots[b], part].astype(F32)
-            next_ref[b * BATCH + r:b * BATCH + r + PIECE, :] = rows.astype(BF16)
+        weight = jnp.broadcast_to(weight_t[:, b:b + 1], (BATCH, 128)).astype(BF16)
+        for c in range(0, MODES, 128):
+            rows = elastic[b, :, c:c + 128] + weight * update[slots[b], :, c:c + 128]
+            next_ref[b * BATCH:(b + 1) * BATCH, c:c + 128] = rows
 
     def sum_up(t):
         sums[t * 16:(t + 1) * 16, :] = mm(members, next_ref[tile_rows(t), :])

time: 31.6 us -> 30 us (0.949)
  Pallas kernels: 30.9 us -> 29.3 us
    pallas_call x1, Pallas kernels: 29.2 us -> 27.6 us  [newton_step(): pl.pallas_call(functools.partial(newton_kernel, devices), name='newton',...]
where the time goes in v4:
time: 30 us
  Pallas kernels  29.3 us (98%)
  between operations  0.64 us (2%)
    pallas_call x1, Pallas kernels, newton_step(): pl.pallas_call(functools.partial(newton_kernel, devices), name='newton',...  27.6 us
    pallas_call x1, Pallas kernels, write_out(): pl.pallas_call(write_kernel, name='write', out_shape=(pltpu.HBM((ROWS, MO...  1.7 us

profile of v4, /device:TPU:1, one launch (start us, length us, event | category | flops | bytes accessed | tf_op | source)
XLA Modules:
  0.0 30.0 jit_solution(15725411479508778292)
XLA Ops:
  0.6 27.6 %newton.1 = (bf16[3072,512]{1,0:T(8,128)(2,1)S(1)}, f32[1,128]{1,0:T(1,128)S(1)}) custom-call(s32[2,24]{1,0:T(2,128)} %bitcast.16, s32[1,3072]{1,0:T(1,128)} %flags_hbm.1, f32[6,1,128]{2,1,0:T(1,128)} %bitcast.15, s32[2,128]{1,0:T(2,128)} %neigh_hbm.1, f32[6,1,512]{2,1,0:T(1,128)} %bitcast.14, bf16[1,512]{1,0:T(2,128)(2,1)} %readout_hbm.1, ...), custom_call_target="tpu_custom_call" | custom-call | tf_op jit(solution)/shard_map/newton/pallas_call | solution.py:285
  28.2 1.7 %write.1 = (bf16[3072,512]{1,0:T(8,128)(2,1)}, f32[1,128]{1,0:T(1,128)}) custom-call(bf16[3072,512]{1,0:T(8,128)(2,1)S(1)} %get-tuple-element.6.next_vmem, f32[1,128]{1,0:T(1,128)S(1)} %get-tuple-element.7.coarse_vmem), custom_call_target="tpu_custom_call" | custom-call | tf_op jit(solution)/shard_map/write/pallas_call | solution.py:266

commit v5 on v4

--- a/solution.py
+++ b/solution.py
@@ -115,9 +115,11 @@
         elastic_of(t, [b for b in range(t * 3, t * 3 + 3) if 0 < b < BATCHES - 1])
 
     stiff_in.wait()
-    for t in range(2):
-        elastic_tile(t)
-    for t in range(2, TILES):
+    for t in range(5):
+        micro_in[t].wait()
+    for t in range(5):
+        elastic_tile(t, False)
+    for t in range(5, TILES):
         micro_in[t].wait()
     for copy in small_in[3:]:
         copy.wait()
@@ -146,7 +148,7 @@
         [(flags_ref[0:1, b * BATCH:(b + 1) * BATCH] * alive[b]).astype(F32) for b in range(BATCHES)]
     ).T
 
-    for t in range(2, TILES):
+    for t in range(5, TILES):
         elastic_tile(t, False)
     inverse_in.start()
 

time: 30 us -> 29.6 us (0.987)
  Pallas kernels: 29.3 us -> 28.9 us
    pallas_call x1, Pallas kernels: 27.6 us -> 27.2 us  [newton_step(): pl.pallas_call(functools.partial(newton_kernel, devices), name='newton',...]
where the time goes in v5:
time: 29.6 us; the launch traced here: 29.5 us
  Pallas kernels  28.9 us (98%)
  between operations  0.64 us (2%)
    pallas_call x1, Pallas kernels, newton_step(): pl.pallas_call(functools.partial(newton_kernel, devices), name='newton',...  27.2 us
    pallas_call x1, Pallas kernels, write_out(): pl.pallas_call(write_kernel, name='write', out_shape=(pltpu.HBM((ROWS, MO...  1.7 us

profile of v5, /device:TPU:1, one launch (start us, length us, event | category | flops | bytes accessed | tf_op | source)
XLA Modules:
  0.0 29.5 jit_solution(5091081346542393005)
XLA Ops:
  0.6 27.2 %newton.1 = (bf16[3072,512]{1,0:T(8,128)(2,1)S(1)}, f32[1,128]{1,0:T(1,128)S(1)}) custom-call(s32[2,24]{1,0:T(2,128)} %bitcast.16, s32[1,3072]{1,0:T(1,128)} %flags_hbm.1, f32[6,1,128]{2,1,0:T(1,128)} %bitcast.15, s32[2,128]{1,0:T(2,128)} %neigh_hbm.1, f32[6,1,512]{2,1,0:T(1,128)} %bitcast.14, bf16[1,512]{1,0:T(2,128)(2,1)} %readout_hbm.1, ...), custom_call_target="tpu_custom_call" | custom-call | tf_op jit(solution)/shard_map/newton/pallas_call | solution.py:287
  27.8 1.7 %write.1 = (bf16[3072,512]{1,0:T(8,128)(2,1)}, f32[1,128]{1,0:T(1,128)}) custom-call(bf16[3072,512]{1,0:T(8,128)(2,1)S(1)} %get-tuple-element.6.next_vmem, f32[1,128]{1,0:T(1,128)S(1)} %get-tuple-element.7.coarse_vmem), custom_call_target="tpu_custom_call" | custom-call | tf_op jit(solution)/shard_map/write/pallas_call | solution.py:268
